TPU v7x, 32 devices: a 4x4x1 block of a 4x4x8 slice. The times are simulated.
32 devices in a mesh: dp: 2 (over z, core), ep: 16 (over x, y).
Axes of the slice: x: 4, y: 4, z: 1, core: 2. Of those that a mesh axis runs over, the one named last changes fastest.
The devices are a block of a 4x4x8 slice.
Arguments:
- x: bfloat16 [2, 16, 256, 3584], P('dp', 'ep'), parts along dimension 0
- expert: int32 [2, 16, 256, 8], P('dp', 'ep'), parts along dimension 0
- slot: int32 [2, 16, 256, 8], P('dp', 'ep'), parts along dimension 0
- gate: float32 [2, 16, 256, 8], P('dp', 'ep'), parts along dimension 0
- w_gate: bfloat16 [48, 3584, 2048], P('ep')
- w_up: bfloat16 [48, 3584, 2048], P('ep')
- w_down: bfloat16 [48, 2048, 3584], P('ep')
- s_gate: bfloat16 [3584, 2048], replicated
- s_up: bfloat16 [3584, 2048], replicated
- s_down: bfloat16 [2048, 3584], replicated
Outputs:
- y: bfloat16 [2, 16, 256, 3584], P('dp', 'ep'), parts along dimension 0
There are 2 independent parts. A program takes and returns all parts, laid end to end along the dimension named above; an argument that names none is the same for every part.
All inputs are finite; a program needn't handle non-finite values.
Results may differ from a plain program's by a relative error of at most 0.009.
Values are sent between devices in bfloat16 or wider.
A program may use at most 768 MiB of HBM per device.

v0:
```python
import jax
import jax.numpy as jnp
from jax import lax
from jax.sharding import NamedSharding, PartitionSpec as P


def einsum(form, a, b):
    return jnp.einsum(form, a.astype(jnp.float32), b.astype(jnp.float32))


def for_all(x, s_gate, s_up, s_down):
    h = jax.nn.silu(einsum("...d,df->...f", x, s_gate)) * einsum("...d,df->...f", x, s_up)
    return einsum("...f,fd->...d", h.astype(jnp.bfloat16), s_down)


def solution(mesh):
    def placed(v, *spec):
        return lax.with_sharding_constraint(v, NamedSharding(mesh, P(*spec)))

    def step(x, expert, slot, gate, w_gate, w_up, w_down, s_gate, s_up, s_down):
        experts, (tokens, top) = w_gate.shape[0], expert.shape[2:]
        slots = 5 * tokens * top // (4 * experts)
        to_expert = jax.nn.one_hot(expert, experts, dtype=jnp.bfloat16)
        to_slot = jax.nn.one_hot(slot, slots, dtype=jnp.bfloat16)
        weighted = to_expert * gate[..., None].astype(jnp.bfloat16)
        dispatch = einsum("abtke,abtkc->abtec", to_expert, to_slot).astype(jnp.bfloat16)
        combine = einsum("abtke,abtkc->abtec", weighted, to_slot).astype(jnp.bfloat16)
        z = einsum("abtec,abtd->aebcd", dispatch, x).astype(jnp.bfloat16)
        z = placed(z, "dp", None, "ep", None, None)
        z = placed(z, "dp", "ep", None, None, None)
        h = jax.nn.silu(einsum("aebcd,edf->aebcf", z, w_gate))
        h = (h * einsum("aebcd,edf->aebcf", z, w_up)).astype(jnp.bfloat16)
        out = einsum("aebcf,efd->aebcd", h, w_down).astype(jnp.bfloat16)
        out = placed(out, "dp", "ep", None, None, None)
        out = placed(out, "dp", None, "ep", None, None)
        y = einsum("abtec,aebcd->abtd", combine, out)
        return (y + for_all(x, s_gate, s_up, s_down)).astype(jnp.bfloat16)

    return step
```

profile of v0, /device:TPU:96, one launch (start us, length us, event | category | flops | bytes accessed | tf_op | source)
XLA Modules:
  0.0 774.0 jit_solution(17910693963812332293)
XLA Ops:
  0.0 0.0 copy-start
  0.0 1.0 copy.11
  1.0 0.0 copy-start.1
  1.0 0.8 copy.9
  1.8 0.0 copy-start.3
  1.8 3.2 convolution_convert_fusion.1
  5.0 0.0 copy-done
  5.0 10.3 %convolution_convert_fusion = bf16[48,53,3584]{2,1,0:T(8,128)(2,1)} fusion(bf16[256,48,53]{2,1,0:T(8,128)(2,1)S(1)} %convolution_convert_fusion.1, bf16[1,1,256,3584]{3,2,1,0:T(8,128)(2,1)S(1)} %copy-done), kind=kOutput, calls=%fused_computation.18 | convolution fusion | flops 4677378048 | bytes 21372928 | tf_op jit(solution)/abtec,abtd->aebcd/dot_general | solution.py:8
  15.4 0.0 copy-done.1
  15.4 0.0 copy-done.3
  15.4 235.0 %all-to-all.4 = bf16[1,16,3,1,53,3584]{5,4,2,3,0,1:T(8,128)(2,1)} all-to-all(bf16[1,16,3,1,53,3584]{5,4,2,3,0,1:T(8,128)(2,1)} %bitcast.121), channel_id=1, replica_groups=mesh['dp'=2,'ep'=16] {'ep'}, dimensions={1} | all-to-all | bytes 36470784 | tf_op jit(solution)/sharding_constraint;jit(solution)/sharding_constraint | solution.py:18
  250.3 47.7 %fusion.2 = f32[3,16,53,2048]{3,2,1,0:T(8,128)} fusion(bf16[3,3584,2048]{2,1,0:T(8,128)(2,1)} %param.5, bf16[1,16,3,1,53,3584]{5,4,2,3,0,1:T(8,128)(2,1)} %all-to-all.4), kind=kOutput, calls=%fused_computation.2 | convolution fusion | flops 37346082816 | bytes 83116032 | tf_op jit(solution)/aebcd,edf->aebcf/dot_general | solution.py:8
  298.0 47.7 %fusion.4 = f32[3,16,53,2048]{3,2,1,0:T(8,128)} fusion(bf16[3,3584,2048]{2,1,0:T(8,128)(2,1)} %param.4, bf16[1,16,3,1,53,3584]{5,4,2,3,0,1:T(8,128)(2,1)} %all-to-all.4), kind=kOutput, calls=%fused_computation.4 | convolution fusion | flops 37346082816 | bytes 83116032 | tf_op jit(solution)/aebcd,edf->aebcf/dot_general | solution.py:8
  345.7 56.2 %convert_bitcast_fusion = bf16[1,3,16,1,53,3584]{5,4,2,1,3,0:T(8,128)(2,1)} fusion(bf16[3,2048,3584]{2,1,0:T(8,128)(2,1)} %param.6, f32[3,16,53,2048]{3,2,1,0:T(8,128)} %fusion.2, f32[3,16,53,2048]{3,2,1,0:T(8,128)} %fusion.4), kind=kOutput, calls=%fused_computation.15 | convolution fusion | flops 37386461184 | bytes 103956480 | tf_op jit(solution)/aebcf,efd->aebcd/dot_general | solution.py:8
  401.9 15.6 %copy.15 = bf16[1,3,16,1,53,3584]{5,4,1,3,0,2:T(8,128)(2,1)} copy(bf16[1,3,16,1,53,3584]{5,4,2,1,3,0:T(8,128)(2,1)} %convert_bitcast_fusion) | data formatting | bytes 36470784 | tf_op jit(solution)/sharding_constraint;jit(solution)/sharding_constraint | solution.py:18
  417.5 5.9 all-to-all-start.1
  423.3 0.0 copy-done.5
  423.4 0.1 copy.10
  423.5 0.0 copy-done.2
  423.5 4.3 convolution_convert_fusion.2
  427.8 8.8 %convolution_bitcast_fusion.2 = f32[1,1,256,2048]{3,2,1,0:T(8,128)} fusion(bf16[3584,2048]{1,0:T(8,128)(2,1)} %param.7, bf16[1,1,256,3584]{3,2,1,0:T(8,128)(2,1)S(1)} %copy-done), kind=kOutput, calls=%fused_computation.28 | convolution fusion | flops 3758096384 | bytes 18612224 | tf_op jit(solution)/...d,df->...f/dot_general | solution.py:8
  436.6 19.8 %fusion.36 = f32[256,3584]{1,0:T(8,128)} fusion(bf16[2048,3584]{1,0:T(8,128)(2,1)} %param.9, bf16[3584,2048]{1,0:T(8,128)(2,1)} %param.8, f32[1,1,256,2048]{3,2,1,0:T(8,128)} %convolution_bitcast_fusion.2, bf16[1,1,256,3584]{3,2,1,0:T(8,128)(2,1)S(1)} %copy-done), kind=kOutput, calls=%fused_computation.41 | convolution fusion | flops 7519338496 | bytes 36962304 | tf_op jit(solution)/...f,fd->...d/dot_general | solution.py:8
  456.4 304.1 %all-to-all-done.1 = bf16[1,3,16,1,53,3584]{5,4,1,3,0,2:T(8,128)(2,1)} async-done(((bf16[1,3,16,1,53,3584]{5,4,1,3,0,2:T(8,128)(2,1)}), bf16[1,3,16,1,53,3584]{5,4,1,3,0,2:T(8,128)(2,1)}, u32[]{:S(2)}, u32[]{:S(2)}) %all-to-all-start.1) | async-done | bytes 18235424 | tf_op jit(solution)/sharding_constraint;jit(solution)/sharding_constraint | solution.py:18
  760.5 13.6 %fusion.20 = bf16[1,1,256,3584]{3,2,1,0:T(8,128)(2,1)} fusion(f32[256,3584]{1,0:T(8,128)} %fusion.36, bf16[48,53,3584]{2,1,0:T(8,128)(2,1)} %bitcast.24, bf16[256,48,53]{2,1,0:T(8,128)(2,1)} %convolution_convert_fusion.2), kind=kOutput, calls=%fused_computation.23 | convolution fusion | flops 4670095360 | bytes 25042944 | tf_op jit(solution)/abtec,aebcd->abtd/dot_general | solution.py:8
  (5 shorter events, 0.0 us)
Async XLA Ops:
  0.0 5.0 copy-start
  1.0 14.4 %copy-start.1 = (s32[256,8]{1,0:T(8,128)}, s32[256,8]{1,0:T(8,128)S(1)}, u32[]{:S(2)}) copy-start(s32[256,8]{1,0:T(8,128)S(1)} %copy.11) | copy-start | bytes 24580
  1.8 13.5 %copy-start.3 = (s32[256,8]{1,0:T(8,128)}, s32[256,8]{1,0:T(8,128)S(1)}, u32[]{:S(2)}) copy-start(s32[256,8]{1,0:T(8,128)S(1)} %copy.9) | copy-start | bytes 24580
  417.5 5.9 copy-start.5
  417.5 6.0 copy-start.2
  417.5 6.0 copy-start.4
  417.5 343.0 %all-to-all-start.1 = ((bf16[1,3,16,1,53,3584]{5,4,1,3,0,2:T(8,128)(2,1)}), bf16[1,3,16,1,53,3584]{5,4,1,3,0,2:T(8,128)(2,1)}, u32[]{:S(2)}, u32[]{:S(2)}) async-start(bf16[1,3,16,1,53,3584]{5,4,1,3,0,2:T(8,128)(2,1)} %copy.15), calls=%async_computation.1 | async-start | bytes 38535168 | tf_op jit(solution)/sharding_constraint;jit(solution)/sharding_constraint | solution.py:18
where the time goes:
time: 774 us
  waiting for transfers between devices  304 us (39%)
  blocking collectives  235 us (30%)
  matrix products  212 us (27%)
  local copies, waits for them, and re-layouts  17.5 us (2%)
    another operation x1, waiting for transfers between devices, placed(): return lax.with_sharding_constraint(v, NamedSharding(mesh, P(*spec)))  304 us
    another operation x1, blocking collectives, placed(): return lax.with_sharding_constraint(v, NamedSharding(mesh, P(*spec)))  235 us
    dot_general x9, matrix products, einsum(): return jnp.einsum(form, a.astype(jnp.float32), b.astype(jnp.float32))  212 us
    another operation x1, local copies, waits for them, and re-layouts, placed(): return lax.with_sharding_constraint(v, NamedSharding(mesh, P(*spec)))  15.6 us
  transfers between devices with their start and end apart: 1, of which 1 were waited for; matrix products, arithmetic and copies ran while one was open for 4% of the time, Pallas kernels for 0%

commit v1 on v0

v1 whole, which is shorter than its diff:
```python
import functools
import math

import jax
import jax.numpy as jnp
from jax import lax
from jax.experimental import pallas as pl
from jax.experimental.pallas import tpu as pltpu
from jax.sharding import PartitionSpec as P

MESH = pl.DeviceIdType.MESH
F32, BF16 = jnp.float32, jnp.bfloat16
ANY = pl.BlockSpec(memory_space=pl.ANY)
DIRS = (1, -1)
HALF = 256
CHUNK = 2 * HALF
WINDOW = 80


def place(side):
    me = lax.axis_index("ep")
    x, y = me // side, me % side

    def at(dx, dy):
        return {"ep": (x + dx + side) % side * side + (y + dy + side) % side}

    def first(half, d):
        return at(d, 0) if half == 0 else at(0, d)

    def second(half, d):
        return at(0, d) if half == 0 else at(d, 0)

    return me, ((y, x), (x, y)), first, second


def meet(side):
    _, _, first, second = place(side)
    barrier = pltpu.get_barrier_semaphore()
    for d in DIRS:
        pl.semaphore_signal(barrier, inc=1, device_id=first(0, d), device_id_type=MESH)
        pl.semaphore_signal(barrier, inc=1, device_id=second(0, d), device_id_type=MESH)
    pl.semaphore_wait(barrier, 4)


def window_of(s, slots):
    return pl.multiple_of(slots * s // 16 * 16, 16)


def up_kernel(side, slots, x_ref, meta_ref, wg_ref, wu_ref, sg_ref, su_ref,
              h_ref, hs_ref, cmb_ref, g_ref, gm_ref,
              acc, z, xs, xown, wbuf, sel, mst, hst, cst,
              snd, rcv, msnd, mrcv, wsem, xsem, osem, hsem, csem, lsem):
    me, pos, first, second = place(side)
    n = side * side
    tokens, depth = x_ref.shape
    width = wg_ref.shape[2]
    chunks = depth // CHUNK
    local = wg_ref.shape[0]
    rows = slots * n

    def gather(c, step, half, di):
        d = DIRS[di]
        o, i = pos[half]
        k = step * 4 + half * 2 + di
        part = pl.ds(0 if di == 0 else tokens // 2, tokens // 2)
        pair = pl.ds(0 if di == 0 else side // 2, side // 2)
        if step == 0:
            src = xown.at[:, pl.ds(pl.multiple_of(c * CHUNK + half * HALF, HALF), HALF)]
            dst = g_ref.at[c, half, o, i]
        elif step == 1:
            src = dst = g_ref.at[c, half, o, (i - d + side) % side, part]
        elif step == 2:
            src = dst = g_ref.at[c, half, o]
        else:
            src = dst = g_ref.at[c, half, (o - d + side) % side, pair]
        return pltpu.make_async_remote_copy(
            src_ref=src, dst_ref=dst, send_sem=snd.at[c, k], recv_sem=rcv.at[c, k],
            device_id=(first if step < 2 else second)(half, d), device_id_type=MESH)

    def each(c, step, act):
        for half in range(2):
            for di in range(2):
                act(gather(c, step, half, di))

    def start(c, step):
        each(c, step, lambda cp: cp.start())

    def landed(c, step):
        each(c, step, lambda cp: cp.wait_recv())

    y, x = pos[0]

    def meta(k):
        di = k % 2
        d = DIRS[di]
        if k < 2:
            src, dst, to = meta_ref, gm_ref.at[y, x], first(0, d)
        elif k == 2:
            src = dst = gm_ref.at[y, (x - 1 + side) % side]
            to = first(0, 1)
        elif k < 5:
            src = dst = gm_ref.at[y]
            to = second(0, DIRS[k - 3])
        else:
            src = dst = gm_ref.at[(y - 1 + side) % side]
            to = second(0, 1)
        return pltpu.make_async_remote_copy(
            src_ref=src, dst_ref=dst, send_sem=msnd.at[k], recv_sem=mrcv.at[k],
            device_id=to, device_id_type=MESH)

    def own(c, half):
        o, i = pos[half]
        return pltpu.make_async_copy(
            xown.at[:, pl.ds(pl.multiple_of(c * CHUNK + half * HALF, HALF), HALF)],
            g_ref.at[c, half, o, i], osem.at[c, half])

    def shared_tile(q):
        ref = (sg_ref, su_ref)[q % 2]
        return pltpu.make_async_copy(ref.at[pl.ds(q // 2 * CHUNK, CHUNK)], wbuf.at[q % 3], wsem.at[q % 3])

    def tile(c, j):
        ref = (wg_ref, wu_ref)[j % 2]
        return pltpu.make_async_copy(
            ref.at[j // 2, pl.ds(pl.multiple_of(c * CHUNK, CHUNK), CHUNK)], wbuf.at[j % 3], wsem.at[j % 3])

    load_x = pltpu.make_async_copy(x_ref, xown, lsem.at[0])
    load_x.start()
    keep_meta = pltpu.make_async_copy(meta_ref, mst.at[y, x], lsem.at[1])
    keep_meta.start()
    for q in range(3):
        shared_tile(q).start()
    meet(side)
    load_x.wait()
    keep_meta.wait()
    put_meta = pltpu.make_async_copy(mst.at[y, x], gm_ref.at[y, x], lsem.at[1])
    put_meta.start()

    for k in range(2):
        meta(k).start()
    start(0, 0)

    @pl.loop(0, chunks)
    def _(c):
        for half in range(2):
            own(c, half).start()

    def shared_piece(kc):
        for m in range(2):
            q = kc * 2 + m
            shared_tile(q).wait()

            @pl.loop(0, width // HALF)
            def _(nb):
                cols = pl.ds(pl.multiple_of(nb * HALF, HALF), HALF)
                into = pl.ds(pl.multiple_of(m * width + nb * HALF, HALF), HALF)
                r = jnp.dot(xown[:, kc * CHUNK:(kc + 1) * CHUNK], wbuf[q % 3, :, cols], preferred_element_type=F32)
                if kc > 0:
                    r = acc[0, :tokens, into] + r
                acc[0, :tokens, into] = r

            if q + 3 < 2 * chunks:
                shared_tile(q + 3).start()

    def finish(e, m_rows, dst_ref):
        def put(b, slot):
            cols = pl.ds(pl.multiple_of(b * HALF, HALF), HALF)
            return pltpu.make_async_copy(hst.at[slot, pl.ds(0, m_rows)], dst_ref.at[:, cols], hsem.at[slot])

        for b in range(width // HALF):
            slot = b % 2
            if b >= 2:
                put(b - 2, slot).wait()
            cols = pl.ds(b * HALF, HALF)
            ups = pl.ds(width + b * HALF, HALF)
            gate = acc[e, :m_rows, cols]
            hst[slot, :m_rows] = (jax.nn.silu(gate) * acc[e, :m_rows, ups]).astype(BF16)
            put(b, slot).start()
        for b in range(width // HALF - 2, width // HALF):
            put(b, b % 2).wait()

    for t in range(6):
        if t > 0:
            start(t, 0)
            landed(t - 1, 0)
            start(t - 1, 1)
        if t == 1:
            for k in range(2):
                meta(k).wait_recv()
            meta(2).start()
        if t >= 2:
            landed(t - 2, 1)
            for half in range(2):
                own(t - 2, half).wait()
            start(t - 2, 2)
        if t == 2:
            put_meta.wait()
            meta(2).wait_recv()
            meta(3).start()
            meta(4).start()
        if t == 3:
            meta(3).wait_recv()
            meta(4).wait_recv()
            meta(5).start()
        if t >= 4:
            landed(t - 4, 2)
            start(t - 4, 3)
        shared_piece(t)
        if t == 4:
            meta(5).wait_recv()
            load_m = pltpu.make_async_copy(gm_ref, mst, lsem.at[1])
            load_m.start()
            load_m.wait()

            @pl.loop(0, n)
            def _(s):
                r = lax.broadcasted_iota(jnp.int32, (tokens, 1), 0)
                e = (r >= WINDOW).astype(jnp.int32) + (r >= 2 * WINDOW).astype(jnp.int32)
                off = (r - e * WINDOW + window_of(s, slots) - slots * s).astype(F32)
                expert = jnp.where(r < local * WINDOW, me * local + e, -1).astype(F32)
                pick = jnp.zeros((tokens, tokens), F32)
                weigh = jnp.zeros((tokens, tokens), F32)
                m = mst.at[s % side, s // side]
                for j in range(m.shape[0] // 3):
                    top = m.shape[0] // 3
                    hit = (m[j:j + 1, :] == expert) & (m[top + j:top + j + 1, :] == off)
                    pick = jnp.where(hit, 1.0, pick)
                    weigh = jnp.where(hit, m[2 * top + j:2 * top + j + 1, :], weigh)
                sel[s] = pick[:local * WINDOW].astype(BF16)
                cst[...] = weigh.T.astype(BF16)
                out = pltpu.make_async_copy(cst, cmb_ref.at[s], csem)
                out.start()
                out.wait()

    for kc in range(6, chunks):
        shared_piece(kc)
    for j in range(3):
        tile(0, j).start()
    finish(0, tokens, hs_ref)

    @pl.loop(0, local * rows // 16)
    def _(r):
        e = r // (rows // 16)
        acc[e, pl.ds(pl.multiple_of(r % (rows // 16) * 16, 16), 16)] = jnp.zeros((16, 2 * width), F32)

    def source(c, s, half):
        o, i = (s % side, s // side) if half == 0 else (s // side, s % side)
        slot = s % 4
        return pltpu.make_async_copy(g_ref.at[c, half, o, i], xs.at[slot, half], xsem.at[slot, half])

    @pl.loop(6, chunks + 6)
    def _(t):
        @pl.when(t < chunks)
        def _():
            start(t, 0)

        @pl.when(t - 1 < chunks)
        def _():
            landed(t - 1, 0)
            start(t - 1, 1)

        @pl.when(t - 2 < chunks)
        def _():
            landed(t - 2, 1)
            for half in range(2):
                own(t - 2, half).wait()
            start(t - 2, 2)

        @pl.when(t - 4 < chunks)
        def _():
            landed(t - 4, 2)
            start(t - 4, 3)

        c = t - 6
        landed(c, 3)
        for s in range(3):
            for half in range(2):
                source(c, s, half).start()

        @pl.loop(0, n)
        def _(s):
            for half in range(2):
                source(c, s, half).wait()

            @pl.when(s + 3 < n)
            def _():
                for half in range(2):
                    source(c, s + 3, half).start()

            for half in range(2):
                cols = pl.ds(half * HALF, HALF)
                r = jnp.dot(sel[s], xs[s % 4, half], preferred_element_type=F32).astype(BF16)
                base = window_of(s, slots)
                for e in range(local):
                    old = z[e, pl.ds(base, 16), cols]
                    new = r[e * WINDOW:(e + 1) * WINDOW]
                    z[e, pl.ds(base, 16), cols] = jnp.where(s > 0, old, jnp.zeros_like(old)) + new[:16]
                    z[e, pl.ds(pl.multiple_of(base + 16, 16), WINDOW - 16), cols] = new[16:]

        for j in range(2 * local):
            e, m = j // 2, j % 2
            tile(c, j).wait()

            @pl.loop(0, width // HALF)
            def _(nb):
                cols = pl.ds(pl.multiple_of(nb * HALF, HALF), HALF)
                into = pl.ds(pl.multiple_of(m * width + nb * HALF, HALF), HALF)
                acc[e, :, into] += jnp.dot(z[e, :rows], wbuf[j % 3, :, cols], preferred_element_type=F32)

            if j + 3 < 2 * local:
                tile(c, j + 3).start()
            else:
                @pl.when(c + 1 < chunks)
                def _():
                    tile(c + 1, j + 3 - 2 * local).start()

    for e in range(local):
        finish(e, rows, h_ref.at[e])

    for k in range(6):
        meta(k).wait_send()

    @pl.loop(0, chunks)
    def _(c):
        for step in range(4):
            each(c, step, lambda cp: cp.wait_send())


def down_kernel(side, slots, h_ref, hs_ref, cmb_ref, wd_ref, sd_ref,
                y_ref, r1, r2, r3, r4,
                hv, hs, cv, wbuf, out, shc, v1, v2, v3, v4, b1, b2, b3, b4, total, yst,
                snd, rcv, wsem, vsem, ysem, lsem):
    me, pos, first, second = place(side)
    tokens = hs_ref.shape[0]
    chunks = y_ref.shape[1] // CHUNK
    local, rows = h_ref.shape[:2]
    half_rows, half_side = tokens // 2, side // 2
    landing, held, sending = (r1, r2, r3, r4), (v1, v2, v3, v4), (b1, b2, b3, b4)
    depth = out.shape[0]

    def key(step, half, di):
        return step * 4 + half * 2 + di

    def hop(c, step, half, di):
        k = key(step, half, di)
        return pltpu.make_async_remote_copy(
            src_ref=sending[step].at[c % 2, half, di], dst_ref=landing[step].at[c, half, di],
            send_sem=snd.at[c, k], recv_sem=rcv.at[c, k],
            device_id=(second if step < 2 else first)(half, DIRS[di]), device_id_type=MESH)

    def fetch(c, step, half, di):
        k = key(step, half, di)
        return pltpu.make_async_copy(landing[step].at[c, half, di], held[step].at[half, di], vsem.at[k])

    def each(act):
        for half in range(2):
            for di in range(2):
                act(half, di)

    def free(c, step):
        @pl.when(c >= 2)
        def _():
            each(lambda half, di: hop(c - 2, step, half, di).wait_send())

    def send(c, step):
        each(lambda half, di: hop(c, step, half, di).start())

    def tile(c, j):
        cols = pl.ds(pl.multiple_of(c * CHUNK, CHUNK), CHUNK)
        src = wd_ref.at[j, :, cols] if j < local else sd_ref.at[:, cols]
        return pltpu.make_async_copy(src, wbuf.at[j % 2], wsem.at[j % 2])

    def term(c, half, o, i):
        s = i * side + o if half == 0 else o * side + i
        base = window_of(s, slots)
        cols = pl.ds(half * HALF, HALF)
        parts = [out[c % depth, e, pl.ds(base, WINDOW), cols] for e in range(local)]
        parts.append(jnp.zeros((tokens - local * WINDOW, HALF), BF16))
        return jnp.dot(cv[s], jnp.concatenate(parts, axis=0), preferred_element_type=F32)

    loads = [pltpu.make_async_copy(h_ref, hv, lsem.at[0]), pltpu.make_async_copy(hs_ref, hs, lsem.at[1]),
             pltpu.make_async_copy(cmb_ref, cv, lsem.at[2])]
    for cp in loads:
        cp.start()
    for j in range(2):
        tile(0, j).start()
    for b in range(depth):
        for e in range(local):
            out[b, e, rows:] = jnp.zeros((out.shape[2] - rows, CHUNK), BF16)
    meet(side)
    for cp in loads:
        cp.wait()

    def y_put(c, half):
        cols = pl.ds(pl.multiple_of(c * CHUNK + half * HALF, HALF), HALF)
        return pltpu.make_async_copy(yst.at[c % 2, half], y_ref.at[:, cols], ysem.at[c % 2, half])

    @pl.loop(0, chunks + 8)
    def _(t):
        for step in range(4):
            c = t - 2 * (step + 1)

            @pl.when((c >= 0) & (c < chunks))
            def _():
                each(lambda half, di: hop(c, step, half, di).wait_recv())
                each(lambda half, di: fetch(c, step, half, di).start())

        @pl.when(t < chunks)
        def _():
            c = t
            for j in range(local + 1):
                tile(c, j).wait()

                @pl.loop(0, 2)
                def _(nb):
                    cols = pl.ds(pl.multiple_of(nb * HALF, HALF), HALF)
                    if j < local:
                        out[c % depth, j, :rows, cols] = jnp.dot(
                            hv[j], wbuf[j % 2, :, cols], preferred_element_type=F32).astype(BF16)
                    else:
                        shc[c, :, cols] = jnp.dot(hs[...], wbuf[j % 2, :, cols], preferred_element_type=F32)

                if j + 2 <= local:
                    tile(c, j + 2).start()
                else:
                    @pl.when(c + 1 < chunks)
                    def _():
                        tile(c + 1, j + 1 - local).start()

            free(c, 0)
            for half in range(2):
                o, i = pos[half]
                for di in range(2):
                    @pl.loop(0, half_side)
                    def _(b):
                        b1[c % 2, half, di, b] = term(c, half, (o + 2) % side, di * half_side + b).astype(BF16)
            send(c, 0)

        @pl.when((t >= 2) & (t - 2 < chunks))
        def _():
            c = t - 2
            each(lambda half, di: fetch(c, 0, half, di).wait())
            free(c, 1)
            for half in range(2):
                o, i = pos[half]
                for di in range(2):
                    to = (o + DIRS[di] + side) % side

                    @pl.loop(0, half_side)
                    def _(b):
                        own = term(c, half, to, di * half_side + b)
                        b2[c % 2, half, di, di * half_side + b] = (own + v1[half, di, b].astype(F32)).astype(BF16)
                        other = (1 - di) * half_side + b
                        b2[c % 2, half, di, other] = term(c, half, to, other).astype(BF16)
            send(c, 1)

        @pl.when((t >= 4) & (t - 4 < chunks))
        def _():
            c = t - 4
            each(lambda half, di: fetch(c, 1, half, di).wait())
            free(c, 2)
            for half in range(2):
                o, i = pos[half]
                for turn in (2, 1, 3, 0):
                    to = (i + turn) % side
                    s = term(c, half, o, to) + v2[half, 0, to].astype(F32) + v2[half, 1, to].astype(F32)
                    if turn == 2:
                        for di in range(2):
                            b3[c % 2, half, di] = s[di * half_rows:(di + 1) * half_rows].astype(BF16)
                    else:
                        total[c % depth, half, min(turn, 2)] = s
            send(c, 2)

        @pl.when((t >= 6) & (t - 6 < chunks))
        def _():
            c = t - 6
            each(lambda half, di: fetch(c, 2, half, di).wait())
            free(c, 3)
            for half in range(2):
                for di in range(2):
                    mine = pl.ds(di * half_rows, half_rows)
                    rest = pl.ds((1 - di) * half_rows, half_rows)
                    b4[c % 2, half, di, mine] = (
                        total[c % depth, half, 1 + di, mine] + v3[half, di].astype(F32)).astype(BF16)
                    b4[c % 2, half, di, rest] = total[c % depth, half, 1 + di, rest].astype(BF16)
            send(c, 3)

        @pl.when(t >= 8)
        def _():
            c = t - 8
            each(lambda half, di: fetch(c, 3, half, di).wait())

            @pl.when(c >= 2)
            def _():
                for half in range(2):
                    y_put(c - 2, half).wait()

            for half in range(2):
                s = total[c % depth, half, 0] + v4[half, 0].astype(F32) + v4[half, 1].astype(F32)
                yst[c % 2, half] = (s + shc[c, :, half * HALF:(half + 1) * HALF]).astype(BF16)
                y_put(c, half).start()

    for c in range(max(chunks - 2, 0), chunks):
        for step in range(4):
            each(lambda half, di: hop(c, step, half, di).wait_send())
        for half in range(2):
            y_put(c, half).wait()


def solution(mesh):
    n = mesh.shape["ep"]
    side = math.isqrt(n)

    def body(x, expert, slot, gate, w_gate, w_up, w_down, s_gate, s_up, s_down):
        x, expert, slot, gate = (v[0, 0] for v in (x, expert, slot, gate))
        tokens, depth = x.shape
        top = expert.shape[1]
        local, _, width = w_gate.shape
        slots = 5 * tokens * top // (4 * local * n)
        chunks = depth // CHUNK
        rows = slots * n
        padded = (slots * (n - 1)) // 16 * 16 + WINDOW
        meta = jnp.concatenate([
            expert.T.astype(F32),
            jnp.where(slot < slots, slot, -1024).T.astype(F32),
            gate.T.astype(BF16).astype(F32),
        ], axis=0)
        dma = pltpu.SemaphoreType.DMA
        h, hs, cmb, _, _ = pl.pallas_call(
            functools.partial(up_kernel, side, slots),
            out_shape=(
                jax.ShapeDtypeStruct((local, rows, width), BF16),
                jax.ShapeDtypeStruct((tokens, width), BF16),
                jax.ShapeDtypeStruct((n, tokens, tokens), BF16),
                jax.ShapeDtypeStruct((chunks, 2, side, side, tokens, HALF), BF16),
                jax.ShapeDtypeStruct((side, side, *meta.shape), F32),
            ),
            in_specs=[ANY] * 6,
            out_specs=(ANY,) * 5,
            scratch_shapes=[
                pltpu.VMEM((local, rows, 2 * width), F32),
                pltpu.VMEM((local, padded, CHUNK), BF16),
                pltpu.VMEM((4, 2, tokens, HALF), BF16),
                pltpu.VMEM((tokens, depth), BF16),
                pltpu.VMEM((3, CHUNK, width), BF16),
                pltpu.VMEM((n, local * WINDOW, tokens), BF16),
                pltpu.VMEM((side, side, *meta.shape), F32),
                pltpu.VMEM((2, rows, HALF), BF16),
                pltpu.VMEM((tokens, tokens), BF16),
                dma((chunks, 16)), dma((chunks, 16)), dma((6,)), dma((6,)), dma((3,)), dma((4, 2)),
                dma((chunks, 2)), dma((2,)), dma(()), dma((2,)),
            ],
            compiler_params=pltpu.CompilerParams(
                collective_id=0, has_side_effects=True, vmem_limit_bytes=67043328),
            name="dispatch_up",
        )(x, meta, w_gate, w_up, s_gate, s_up)
        y = pl.pallas_call(
            functools.partial(down_kernel, side, slots),
            out_shape=(
                jax.ShapeDtypeStruct((tokens, depth), BF16),
                jax.ShapeDtypeStruct((chunks, 2, 2, side // 2, tokens, HALF), BF16),
                jax.ShapeDtypeStruct((chunks, 2, 2, side, tokens, HALF), BF16),
                jax.ShapeDtypeStruct((chunks, 2, 2, tokens // 2, HALF), BF16),
                jax.ShapeDtypeStruct((chunks, 2, 2, tokens, HALF), BF16),
            ),
            in_specs=[ANY] * 5,
            out_specs=(ANY,) * 5,
            scratch_shapes=[
                pltpu.VMEM((local, rows, width), BF16),
                pltpu.VMEM((tokens, width), BF16),
                pltpu.VMEM((n, tokens, tokens), BF16),
                pltpu.VMEM((2, width, CHUNK), BF16),
                pltpu.VMEM((5, local, padded, CHUNK), BF16),
                pltpu.VMEM((chunks, tokens, CHUNK), F32),
                pltpu.VMEM((2, 2, side // 2, tokens, HALF), BF16),
                pltpu.VMEM((2, 2, side, tokens, HALF), BF16),
                pltpu.VMEM((2, 2, tokens // 2, HALF), BF16),
                pltpu.VMEM((2, 2, tokens, HALF), BF16),
                pltpu.VMEM((2, 2, 2, side // 2, tokens, HALF), BF16),
                pltpu.VMEM((2, 2, 2, side, tokens, HALF), BF16),
                pltpu.VMEM((2, 2, 2, tokens // 2, HALF), BF16),
                pltpu.VMEM((2, 2, 2, tokens, HALF), BF16),
                pltpu.VMEM((5, 2, 3, tokens, HALF), F32),
                pltpu.VMEM((2, 2, tokens, HALF), BF16),
                dma((chunks, 16)), dma((chunks, 16)), dma((2,)), dma((16,)), dma((2, 2)), dma((3,)),
            ],
            compiler_params=pltpu.CompilerParams(
                collective_id=1, has_side_effects=True, vmem_limit_bytes=67043328),
            name="down_combine",
        )(h, hs, cmb, w_down, s_down)[0]
        return y[None, None]

    token, expert, whole = P("dp", "ep", None, None), P("ep", None, None), P(None, None)
    return jax.shard_map(
        body,
        mesh=mesh,
        in_specs=(token,) * 4 + (expert,) * 3 + (whole,) * 3,
        out_specs=token,
        check_vma=False,
    )
```

time: 774 us -> 465 us (0.60)
  Pallas kernels: 0 us -> 458 us
  waiting for transfers between devices: 304 us -> 0 us
  blocking collectives: 235 us -> 0 us
  matrix products: 212 us -> 0 us
  local copies, waits for them, and re-layouts: 17.5 us -> 2.85 us
    pallas_call x0 -> x2, Pallas kernels: none -> 458 us  [the longest x1 283 us: body(): pl.pallas_call(functools.partial(up_kernel, side, slots), out_shape=(jax....]
    another operation x1 -> x0, waiting for transfers between devices: 304 us -> none  [placed(): return lax.with_sharding_constraint(v, NamedSharding(mesh, P(*spec)))]
    another operation x1 -> x0, blocking collectives: 235 us -> none  [placed(): return lax.with_sharding_constraint(v, NamedSharding(mesh, P(*spec)))]
    dot_general x9 -> x0, matrix products: 212 us -> none  [einsum(): return jnp.einsum(form, a.astype(jnp.float32), b.astype(jnp.float32))]
    another operation x1 -> x0, local copies, waits for them, and re-layouts: 15.6 us -> none  [placed(): return lax.with_sharding_constraint(v, NamedSharding(mesh, P(*spec)))]
  transfers between devices with their start and end apart: 1 -> 0, of which waited for: 1 -> 0; matrix products, arithmetic and copies ran while one was open for 4% -> 0% of each run, Pallas kernels for 0% -> 0%
where the time goes in v1:
time: 465 us; the launch traced here: 464 us
  Pallas kernels  458 us (98%)
    pallas_call x1, Pallas kernels, body(): pl.pallas_call(functools.partial(up_kernel, side, slots), out_shape=(jax....  283 us
    pallas_call x1, Pallas kernels, body(): pl.pallas_call(functools.partial(down_kernel, side, slots), out_shape=(ja...  175 us

profile of v1, /device:TPU:96, one launch (start us, length us, event | category | flops | bytes accessed | tf_op | source)
XLA Modules:
  0.0 463.6 jit_solution(10877638501267751308)
XLA Ops:
  0.0 0.7 convert_bitcast_fusion.1
  0.7 0.7 fusion.1
  1.4 0.7 convert_bitcast_fusion
  2.1 0.6 pad_maximum_fusion.meta_ref
  2.7 282.9 %dispatch_up.1 = (bf16[3,848,2048]{2,1,0:T(8,128)(2,1)}, bf16[256,2048]{1,0:T(8,128)(2,1)}, bf16[16,256,256]{2,1,0:T(8,128)(2,1)}, bf16[7,2,4,4,256,256]{5,4,3,2,1,0:T(8,128)(2,1)}, f32[4,4,24,256]{3,2,1,0:T(8,128)}) custom-call(bf16[256,3584]{1,0:T(8,128)(2,1)} %bitcast.15, f32[24,256]{1,0:T(8,128)} %pad_maximum_fusion.meta_ref, ...), custom_call_target="tpu_custom_call" | custom-call | tf_op jit(solution)/shard_map/dispatch_up/pallas_call | solution.py:528
  285.6 175.1 %down_combine.1 = (bf16[256,3584]{1,0:T(8,128)(2,1)}, bf16[7,2,2,2,256,256]{5,4,3,2,1,0:T(8,128)(2,1)}, bf16[7,2,2,4,256,256]{5,4,3,2,1,0:T(8,128)(2,1)}, bf16[7...) custom-call(bf16[3,848,2048]{2,1,0:T(8,128)(2,1)} %get-tuple-element.9.h_ref, ...), custom_call_target="tpu_custom_call" | custom-call | tf_op jit(solution)/shard_map/down_combine/pallas_call | solution.py:556
  460.8 2.8 copy.12

commit v2 on v1

--- a/solution.py
+++ b/solution.py
@@ -14,6 +14,7 @@
 DIRS = (1, -1)
 HALF = 256
 CHUNK = 2 * HALF
+WIDE = 1024
 WINDOW = 80
 
 
@@ -118,10 +119,11 @@
         ref = (sg_ref, su_ref)[q % 2]
         return pltpu.make_async_copy(ref.at[pl.ds(q // 2 * CHUNK, CHUNK)], wbuf.at[q % 3], wsem.at[q % 3])
 
-    def tile(c, j):
-        ref = (wg_ref, wu_ref)[j % 2]
+    def tile(c, e, m):
+        slot = (2 * e + m) % 3
+        ref = (wg_ref, wu_ref)[m]
         return pltpu.make_async_copy(
-            ref.at[j // 2, pl.ds(pl.multiple_of(c * CHUNK, CHUNK), CHUNK)], wbuf.at[j % 3], wsem.at[j % 3])
+            ref.at[e, pl.ds(pl.multiple_of(c * CHUNK, CHUNK), CHUNK)], wbuf.at[slot], wsem.at[slot])
 
     load_x = pltpu.make_async_copy(x_ref, xown, lsem.at[0])
     load_x.start()
@@ -137,7 +139,6 @@
 
     for k in range(2):
         meta(k).start()
-    start(0, 0)
 
     @pl.loop(0, chunks)
     def _(c):
@@ -149,10 +150,10 @@
             q = kc * 2 + m
             shared_tile(q).wait()
 
-            @pl.loop(0, width // HALF)
+            @pl.loop(0, width // WIDE)
             def _(nb):
-                cols = pl.ds(pl.multiple_of(nb * HALF, HALF), HALF)
-                into = pl.ds(pl.multiple_of(m * width + nb * HALF, HALF), HALF)
+                cols = pl.ds(pl.multiple_of(nb * WIDE, WIDE), WIDE)
+                into = pl.ds(pl.multiple_of(m * width + nb * WIDE, WIDE), WIDE)
                 r = jnp.dot(xown[:, kc * CHUNK:(kc + 1) * CHUNK], wbuf[q % 3, :, cols], preferred_element_type=F32)
                 if kc > 0:
                     r = acc[0, :tokens, into] + r
@@ -178,20 +179,39 @@
         for b in range(width // HALF - 2, width // HALF):
             put(b, b % 2).wait()
 
+    def exchange(t, at):
+        at(t, lambda c: start(c, 0))
+
+        def second_step(c):
+            landed(c, 0)
+            start(c, 1)
+
+        def third_step(c):
+            landed(c, 1)
+            for half in range(2):
+                own(c, half).wait()
+            start(c, 2)
+
+        def fourth_step(c):
+            landed(c, 2)
+            start(c, 3)
+
+        at(t - 1, second_step)
+        at(t - 5, fourth_step)
+        at(t - 3, third_step)
+
+    def if_static(c, act):
+        if 0 <= c < chunks:
+            act(c)
+
+    def if_traced(c, act):
+        pl.when(c < chunks)(lambda: act(c))
+
     for t in range(6):
-        if t > 0:
-            start(t, 0)
-            landed(t - 1, 0)
-            start(t - 1, 1)
         if t == 1:
             for k in range(2):
                 meta(k).wait_recv()
             meta(2).start()
-        if t >= 2:
-            landed(t - 2, 1)
-            for half in range(2):
-                own(t - 2, half).wait()
-            start(t - 2, 2)
         if t == 2:
             put_meta.wait()
             meta(2).wait_recv()
@@ -201,40 +221,47 @@
             meta(3).wait_recv()
             meta(4).wait_recv()
             meta(5).start()
-        if t >= 4:
-            landed(t - 4, 2)
-            start(t - 4, 3)
+        exchange(t, if_static)
         shared_piece(t)
-        if t == 4:
-            meta(5).wait_recv()
-            load_m = pltpu.make_async_copy(gm_ref, mst, lsem.at[1])
-            load_m.start()
-            load_m.wait()
-
-            @pl.loop(0, n)
-            def _(s):
-                r = lax.broadcasted_iota(jnp.int32, (tokens, 1), 0)
-                e = (r >= WINDOW).astype(jnp.int32) + (r >= 2 * WINDOW).astype(jnp.int32)
-                off = (r - e * WINDOW + window_of(s, slots) - slots * s).astype(F32)
-                expert = jnp.where(r < local * WINDOW, me * local + e, -1).astype(F32)
-                pick = jnp.zeros((tokens, tokens), F32)
-                weigh = jnp.zeros((tokens, tokens), F32)
-                m = mst.at[s % side, s // side]
-                for j in range(m.shape[0] // 3):
-                    top = m.shape[0] // 3
-                    hit = (m[j:j + 1, :] == expert) & (m[top + j:top + j + 1, :] == off)
-                    pick = jnp.where(hit, 1.0, pick)
-                    weigh = jnp.where(hit, m[2 * top + j:2 * top + j + 1, :], weigh)
-                sel[s] = pick[:local * WINDOW].astype(BF16)
-                cst[...] = weigh.T.astype(BF16)
-                out = pltpu.make_async_copy(cst, cmb_ref.at[s], csem)
-                out.start()
-                out.wait()
+
+    meta(5).wait_recv()
+    load_m = pltpu.make_async_copy(gm_ref, mst, lsem.at[1])
+    load_m.start()
+    load_m.wait()
+
+    def put_weights(s):
+        return pltpu.make_async_copy(cst.at[s % 2], cmb_ref.at[s], csem.at[s % 2])
+
+    @pl.loop(0, n)
+    def _(s):
+        r = lax.broadcasted_iota(jnp.int32, (tokens, 1), 0)
+        e = (r >= WINDOW).astype(jnp.int32) + (r >= 2 * WINDOW).astype(jnp.int32)
+        off = (r - e * WINDOW + window_of(s, slots) - slots * s).astype(F32)
+        expert = jnp.where(r < local * WINDOW, me * local + e, -1).astype(F32)
+        pick = jnp.zeros((tokens, tokens), F32)
+        weigh = jnp.zeros((tokens, tokens), F32)
+        m = mst.at[s % side, s // side]
+        top = m.shape[0] // 3
+        for j in range(top):
+            hit = (m[j:j + 1, :] == expert) & (m[top + j:top + j + 1, :] == off)
+            pick = jnp.where(hit, 1.0, pick)
+            weigh = jnp.where(hit, m[2 * top + j:2 * top + j + 1, :], weigh)
+        sel[s] = pick[:local * WINDOW].astype(BF16)
+
+        @pl.when(s >= 2)
+        def _():
+            put_weights(s - 2).wait()
+
+        cst[s % 2] = weigh.T.astype(BF16)
+        put_weights(s).start()
+
+    for s in range(n - 2, n):
+        put_weights(s).wait()
 
     for kc in range(6, chunks):
         shared_piece(kc)
     for j in range(3):
-        tile(0, j).start()
+        tile(0, j // 2, j % 2).start()
     finish(0, tokens, hs_ref)
 
     @pl.loop(0, local * rows // 16)
@@ -242,76 +269,59 @@
         e = r // (rows // 16)
         acc[e, pl.ds(pl.multiple_of(r % (rows // 16) * 16, 16), 16)] = jnp.zeros((16, 2 * width), F32)
 
-    def source(c, s, half):
-        o, i = (s % side, s // side) if half == 0 else (s // side, s % side)
-        slot = s % 4
-        return pltpu.make_async_copy(g_ref.at[c, half, o, i], xs.at[slot, half], xsem.at[slot, half])
+    def source(c, q, half):
+        src = g_ref.at[c, half, :, q] if half == 0 else g_ref.at[c, half, q]
+        return pltpu.make_async_copy(src, xs.at[q, half], xsem.at[q, half])
 
     @pl.loop(6, chunks + 6)
     def _(t):
-        @pl.when(t < chunks)
-        def _():
-            start(t, 0)
-
-        @pl.when(t - 1 < chunks)
-        def _():
-            landed(t - 1, 0)
-            start(t - 1, 1)
-
-        @pl.when(t - 2 < chunks)
-        def _():
-            landed(t - 2, 1)
-            for half in range(2):
-                own(t - 2, half).wait()
-            start(t - 2, 2)
-
-        @pl.when(t - 4 < chunks)
-        def _():
-            landed(t - 4, 2)
-            start(t - 4, 3)
-
+        exchange(t, if_traced)
         c = t - 6
         landed(c, 3)
-        for s in range(3):
-            for half in range(2):
-                source(c, s, half).start()
-
-        @pl.loop(0, n)
-        def _(s):
-            for half in range(2):
-                source(c, s, half).wait()
-
-            @pl.when(s + 3 < n)
-            def _():
-                for half in range(2):
-                    source(c, s + 3, half).start()
+        for q in range(side):
+            for half in range(2):
+                source(c, q, half).start()
+
+        @pl.loop(0, side)
+        def _(q):
+            for half in range(2):
+                source(c, q, half).wait()
 
             for half in range(2):
                 cols = pl.ds(half * HALF, HALF)
-                r = jnp.dot(sel[s], xs[s % 4, half], preferred_element_type=F32).astype(BF16)
-                base = window_of(s, slots)
-                for e in range(local):
-                    old = z[e, pl.ds(base, 16), cols]
-                    new = r[e * WINDOW:(e + 1) * WINDOW]
-                    z[e, pl.ds(base, 16), cols] = jnp.where(s > 0, old, jnp.zeros_like(old)) + new[:16]
-                    z[e, pl.ds(pl.multiple_of(base + 16, 16), WINDOW - 16), cols] = new[16:]
-
-        for j in range(2 * local):
-            e, m = j // 2, j % 2
-            tile(c, j).wait()
-
-            @pl.loop(0, width // HALF)
-            def _(nb):
-                cols = pl.ds(pl.multiple_of(nb * HALF, HALF), HALF)
-                into = pl.ds(pl.multiple_of(m * width + nb * HALF, HALF), HALF)
-                acc[e, :, into] += jnp.dot(z[e, :rows], wbuf[j % 3, :, cols], preferred_element_type=F32)
-
-            if j + 3 < 2 * local:
-                tile(c, j + 3).start()
-            else:
-                @pl.when(c + 1 < chunks)
+                for b in range(side):
+                    s = q * side + b
+                    r = jnp.dot(sel[s], xs[q, half, b], preferred_element_type=F32).astype(BF16)
+                    base = window_of(s, slots)
+                    for e in range(local):
+                        new = r[e * WINDOW:(e + 1) * WINDOW]
+                        old = z[e, pl.ds(base, 16), cols]
+                        if b == 0:
+                            old = jnp.where(q > 0, old, jnp.zeros_like(old))
+                        z[e, pl.ds(base, 16), cols] = old + new[:16]
+                        z[e, pl.ds(pl.multiple_of(base + 16, 16), WINDOW - 16), cols] = new[16:]
+
+        @pl.loop(0, local)
+        def _(e):
+            for m in range(2):
+                slot = (2 * e + m) % 3
+                tile(c, e, m).wait()
+
+                @pl.loop(0, width // WIDE)
+                def _(nb):
+                    cols = pl.ds(pl.multiple_of(nb * WIDE, WIDE), WIDE)
+                    into = pl.ds(pl.multiple_of(m * width + nb * WIDE, WIDE), WIDE)
+                    acc[e, :, into] += jnp.dot(z[e, :rows], wbuf[slot, :, cols], preferred_element_type=F32)
+
+                later = e + 1 + m
+
+                @pl.when(later < local)
                 def _():
-                    tile(c + 1, j + 3 - 2 * local).start()
+                    tile(c, later, 1 - m).start()
+
+                @pl.when((later >= local) & (c + 1 < chunks))
+                def _():
+                    tile(c + 1, later - local, 1 - m).start()
 
     for e in range(local):
         finish(e, rows, h_ref.at[e])
@@ -377,27 +387,26 @@
         parts.append(jnp.zeros((tokens - local * WINDOW, HALF), BF16))
         return jnp.dot(cv[s], jnp.concatenate(parts, axis=0), preferred_element_type=F32)
 
-    loads = [pltpu.make_async_copy(h_ref, hv, lsem.at[0]), pltpu.make_async_copy(hs_ref, hs, lsem.at[1]),
-             pltpu.make_async_copy(cmb_ref, cv, lsem.at[2])]
-    for cp in loads:
-        cp.start()
+    loads = [pltpu.make_async_copy(h_ref.at[e], hv.at[e], lsem.at[e]) for e in range(local)]
+    loads += [pltpu.make_async_copy(hs_ref, hs, lsem.at[local]), pltpu.make_async_copy(cmb_ref, cv, lsem.at[local + 1])]
+    loads[0].start()
     for j in range(2):
         tile(0, j).start()
+    for cp in loads[1:]:
+        cp.start()
     for b in range(depth):
         for e in range(local):
             out[b, e, rows:] = jnp.zeros((out.shape[2] - rows, CHUNK), BF16)
     meet(side)
-    for cp in loads:
-        cp.wait()
 
     def y_put(c, half):
         cols = pl.ds(pl.multiple_of(c * CHUNK + half * HALF, HALF), HALF)
         return pltpu.make_async_copy(yst.at[c % 2, half], y_ref.at[:, cols], ysem.at[c % 2, half])
 
-    @pl.loop(0, chunks + 8)
+    @pl.loop(0, chunks + 7)
     def _(t):
-        for step in range(4):
-            c = t - 2 * (step + 1)
+        for step in range(1, 4):
+            c = t - 2 * step - 1
 
             @pl.when((c >= 0) & (c < chunks))
             def _():
@@ -409,6 +418,10 @@
             c = t
             for j in range(local + 1):
                 tile(c, j).wait()
+
+                @pl.when(c == 0)
+                def _():
+                    loads[j].wait()
 
                 @pl.loop(0, 2)
                 def _(nb):
@@ -426,6 +439,19 @@
                     def _():
                         tile(c + 1, j + 1 - local).start()
 
+        @pl.when((t >= 1) & (t - 1 < chunks))
+        def _():
+            each(lambda half, di: hop(t - 1, 0, half, di).wait_recv())
+            each(lambda half, di: fetch(t - 1, 0, half, di).start())
+
+        @pl.when(t < chunks)
+        def _():
+            c = t
+
+            @pl.when(c == 0)
+            def _():
+                loads[local + 1].wait()
+
             free(c, 0)
             for half in range(2):
                 o, i = pos[half]
@@ -435,9 +461,9 @@
                         b1[c % 2, half, di, b] = term(c, half, (o + 2) % side, di * half_side + b).astype(BF16)
             send(c, 0)
 
-        @pl.when((t >= 2) & (t - 2 < chunks))
-        def _():
-            c = t - 2
+        @pl.when((t >= 1) & (t - 1 < chunks))
+        def _():
+            c = t - 1
             each(lambda half, di: fetch(c, 0, half, di).wait())
             free(c, 1)
             for half in range(2):
@@ -453,9 +479,9 @@
                         b2[c % 2, half, di, other] = term(c, half, to, other).astype(BF16)
             send(c, 1)
 
-        @pl.when((t >= 4) & (t - 4 < chunks))
-        def _():
-            c = t - 4
+        @pl.when((t >= 3) & (t - 3 < chunks))
+        def _():
+            c = t - 3
             each(lambda half, di: fetch(c, 1, half, di).wait())
             free(c, 2)
             for half in range(2):
@@ -470,9 +496,9 @@
                         total[c % depth, half, min(turn, 2)] = s
             send(c, 2)
 
-        @pl.when((t >= 6) & (t - 6 < chunks))
-        def _():
-            c = t - 6
+        @pl.when((t >= 5) & (t - 5 < chunks))
+        def _():
+            c = t - 5
             each(lambda half, di: fetch(c, 2, half, di).wait())
             free(c, 3)
             for half in range(2):
@@ -484,9 +510,9 @@
                     b4[c % 2, half, di, rest] = total[c % depth, half, 1 + di, rest].astype(BF16)
             send(c, 3)
 
-        @pl.when(t >= 8)
-        def _():
-            c = t - 8
+        @pl.when(t >= 7)
+        def _():
+            c = t - 7
             each(lambda half, di: fetch(c, 3, half, di).wait())
 
             @pl.when(c >= 2)
@@ -539,15 +565,15 @@
             scratch_shapes=[
                 pltpu.VMEM((local, rows, 2 * width), F32),
                 pltpu.VMEM((local, padded, CHUNK), BF16),
-                pltpu.VMEM((4, 2, tokens, HALF), BF16),
+                pltpu.VMEM((side, 2, side, tokens, HALF), BF16),
                 pltpu.VMEM((tokens, depth), BF16),
                 pltpu.VMEM((3, CHUNK, width), BF16),
                 pltpu.VMEM((n, local * WINDOW, tokens), BF16),
                 pltpu.VMEM((side, side, *meta.shape), F32),
                 pltpu.VMEM((2, rows, HALF), BF16),
-                pltpu.VMEM((tokens, tokens), BF16),
-                dma((chunks, 16)), dma((chunks, 16)), dma((6,)), dma((6,)), dma((3,)), dma((4, 2)),
-                dma((chunks, 2)), dma((2,)), dma(()), dma((2,)),
+                pltpu.VMEM((2, tokens, tokens), BF16),
+                dma((chunks, 16)), dma((chunks, 16)), dma((6,)), dma((6,)), dma((3,)), dma((side, 2)),
+                dma((chunks, 2)), dma((2,)), dma((2,)), dma((2,)),
             ],
             compiler_params=pltpu.CompilerParams(
                 collective_id=0, has_side_effects=True, vmem_limit_bytes=67043328),
@@ -581,7 +607,7 @@
                 pltpu.VMEM((2, 2, 2, tokens, HALF), BF16),
                 pltpu.VMEM((5, 2, 3, tokens, HALF), F32),
                 pltpu.VMEM((2, 2, tokens, HALF), BF16),
-                dma((chunks, 16)), dma((chunks, 16)), dma((2,)), dma((16,)), dma((2, 2)), dma((3,)),
+                dma((chunks, 16)), dma((chunks, 16)), dma((2,)), dma((16,)), dma((2, 2)), dma((local + 2,)),
             ],
             compiler_params=pltpu.CompilerParams(
                 collective_id=1, has_side_effects=True, vmem_limit_bytes=67043328),

time: 465 us -> 381 us (0.82)
  Pallas kernels: 458 us -> 375 us
    pallas_call x1, Pallas kernels: 283 us -> 204 us  [body(): pl.pallas_call(functools.partial(up_kernel, side, slots), out_shape=(jax....]
where the time goes in v2:
time: 381 us; the launch traced here: 380 us
  Pallas kernels  375 us (98%)
    pallas_call x1, Pallas kernels, body(): pl.pallas_call(functools.partial(up_kernel, side, slots), out_shape=(jax....  204 us
    pallas_call x1, Pallas kernels, body(): pl.pallas_call(functools.partial(down_kernel, side, slots), out_shape=(ja...  171 us

profile of v2, /device:TPU:96, one launch (start us, length us, event | category | flops | bytes accessed | tf_op | source)
XLA Modules:
  0.0 380.2 jit_solution(4020582631786671517)
XLA Ops:
  0.0 0.7 convert_bitcast_fusion.1
  0.7 0.7 fusion.1
  1.4 0.7 convert_bitcast_fusion
  2.1 0.6 pad_maximum_fusion.meta_ref
  2.7 204.1 %dispatch_up.1 = (bf16[3,848,2048]{2,1,0:T(8,128)(2,1)}, bf16[256,2048]{1,0:T(8,128)(2,1)}, bf16[16,256,256]{2,1,0:T(8,128)(2,1)}, bf16[7,2,4,4,256,256]{5,4,3,2,1,0:T(8,128)(2,1)}, f32[4,4,24,256]{3,2,1,0:T(8,128)}) custom-call(bf16[256,3584]{1,0:T(8,128)(2,1)} %bitcast.15, f32[24,256]{1,0:T(8,128)} %pad_maximum_fusion.meta_ref, ...), custom_call_target="tpu_custom_call" | custom-call | tf_op jit(solution)/shard_map/dispatch_up/pallas_call | solution.py:554
  206.8 170.5 %down_combine.1 = (bf16[256,3584]{1,0:T(8,128)(2,1)}, bf16[7,2,2,2,256,256]{5,4,3,2,1,0:T(8,128)(2,1)}, bf16[7,2,2,4,256,256]{5,4,3,2,1,0:T(8,128)(2,1)}, bf16[7...) custom-call(bf16[3,848,2048]{2,1,0:T(8,128)(2,1)} %get-tuple-element.9.h_ref, ...), custom_call_target="tpu_custom_call" | custom-call | tf_op jit(solution)/shard_map/down_combine/pallas_call | solution.py:582
  377.3 2.8 copy.12
